TPU v7x, 32 devices: a whole 2x2x4 slice. The times are simulated.
32 devices in a mesh: gx: 4 (over y, core), gy: 4 (over z), gz: 2 (over x).
Axes of the slice: x: 2, y: 2, z: 4, core: 2. Of those that a mesh axis runs over, the one named last changes fastest.
Arguments:
- stream: bfloat16 [8192, 8192], P(('gx', 'gy', 'gz')), may hold values from -4 to 4
- segment_ids: int32 [8192], P(('gx', 'gy', 'gz')), may hold values from 0 to 8191, as said below
- positions: int32 [8192], P(('gx', 'gy', 'gz')), may hold values from 0 to 255, as said below
- norm_gain: bfloat16 [1, 8192], P(None, ('gx', 'gy', 'gz')), may hold values from 0.099609375 to 1.8984375
- q_weight: bfloat16 [1, 8192, 512], P(None, ('gx', 'gy', 'gz')), as said below
- k_weight: bfloat16 [1, 8192, 128], P(None, ('gx', 'gy', 'gz')), as said below
- v_weight: bfloat16 [1, 8192, 128], P(None, ('gx', 'gy', 'gz')), may hold values from -0.0625 to 0.0625
- o_weight: bfloat16 [1, 512, 8192], P(None, None, ('gx', 'gy', 'gz')), may hold values from -0.25 to 0.25
Outputs:
- result: bfloat16 [8192, 8192], P(('gx', 'gy', 'gz'))
Inputs may be any that keep to these rules, and one draw needn't show every extreme that they name: `segment_ids`: each token's id is the index of its document's first token, so ids never fall along the tokens; every document lies inside one aligned block of 256 tokens, every block starts a new document, and the last token is a document of its own. `positions`: counts from 0 at a document's first token and rises by one per token. `q_weight`: A projection scaled by its fan-in. `k_weight`: A projection scaled by its fan-in.
All inputs are finite; a program needn't handle non-finite values.
Results may differ from a plain program's by a relative error of at most 0.0064.
Values may be sent and summed in bfloat16 or wider, within the bound.
A program may use at most 128 MiB of HBM per device.

v0:
```python
import math
import jax
import jax.numpy as jnp
from jax import lax
from jax.sharding import PartitionSpec as P


def rotate(values, positions):
    width = values.shape[-1]
    half = width // 2
    freqs = jnp.exp(-math.log(500000.0) * jnp.arange(half, dtype=jnp.float32) * 2.0 / width)
    angles = positions.astype(jnp.float32)[:, None] * freqs[None, :]
    cosine = jnp.concatenate([jnp.cos(angles), jnp.cos(angles)], -1)[:, None, :]
    sine = jnp.concatenate([jnp.sin(angles), jnp.sin(angles)], -1)[:, None, :]
    turned = jnp.concatenate([-values[..., half:], values[..., :half]], -1)
    return values * cosine + turned * sine


def attend(queries, keys, values, segment_ids, positions):
    count = queries.shape[0]
    scores = jnp.einsum(
        "thd,sd->hts", queries, keys, preferred_element_type=jnp.float32
    ) / math.sqrt(keys.shape[-1])
    allowed = (segment_ids[:, None] == segment_ids[None, :]) & (
        positions[None, :] <= positions[:, None]
    )
    scores = jnp.where(allowed[None], scores, -1e30)
    peak = jnp.max(scores, -1, keepdims=True)
    expd = jnp.exp(scores - peak)
    probs = (expd / jnp.sum(expd, -1, keepdims=True)).astype(jnp.bfloat16)
    mixed = jnp.einsum("hts,sd->thd", probs, values, preferred_element_type=jnp.float32)
    return mixed.astype(jnp.bfloat16).reshape(count, -1)


def body(stream, segment_ids, positions, norm_gain, q_weight, k_weight, v_weight, o_weight):
    count = stream.shape[0]
    head_size = k_weight.shape[2]
    current = stream
    widened = lax.optimization_barrier(current).astype(jnp.float32)
    inverse = lax.rsqrt(jnp.mean(widened * widened, -1, keepdims=True) + 1e-05)
    scaled = widened * inverse
    inner = (
        lax.all_gather(norm_gain[0], "gz", axis=0, tiled=True),
        lax.all_gather(q_weight[0], "gz", axis=0, tiled=True),
        lax.all_gather(k_weight[0], "gz", axis=0, tiled=True),
        lax.all_gather(v_weight[0], "gz", axis=0, tiled=True),
    )
    middle = (
        lax.all_gather(inner[0], "gy", axis=0, tiled=True),
        lax.all_gather(inner[1], "gy", axis=0, tiled=True),
        lax.all_gather(inner[2], "gy", axis=0, tiled=True),
        lax.all_gather(inner[3], "gy", axis=0, tiled=True),
    )
    gain_piece = lax.all_gather(middle[0], "gx", axis=0, tiled=True)
    query_piece = lax.all_gather(middle[1], "gx", axis=0, tiled=True)
    key_piece = lax.all_gather(middle[2], "gx", axis=0, tiled=True)
    value_piece = lax.all_gather(middle[3], "gx", axis=0, tiled=True)
    normed = (scaled * gain_piece.astype(jnp.float32)[None, :]).astype(jnp.bfloat16)
    query_raw = jnp.dot(normed, query_piece, preferred_element_type=jnp.float32)
    key_raw = jnp.dot(normed, key_piece, preferred_element_type=jnp.float32)
    value_raw = jnp.dot(normed, value_piece, preferred_element_type=jnp.float32)
    queries = rotate(query_raw.reshape(count, -1, head_size), positions).astype(jnp.bfloat16)
    keys = rotate(key_raw[:, None, :], positions)[:, 0, :].astype(jnp.bfloat16)
    values = value_raw.astype(jnp.bfloat16)
    mixed = attend(queries, keys, values, segment_ids, positions)
    inner_cols = lax.all_gather(o_weight[0], "gz", axis=1, tiled=True)
    middle_cols = lax.all_gather(inner_cols, "gy", axis=1, tiled=True)
    branch = jnp.dot(
        mixed,
        lax.all_gather(middle_cols, "gx", axis=1, tiled=True),
        preferred_element_type=jnp.float32,
    )
    current = (widened + branch).astype(jnp.bfloat16)
    return current


def solution(mesh):
    in_specs = (
        P(("gx", "gy", "gz"), None),
        P(("gx", "gy", "gz")),
        P(("gx", "gy", "gz")),
        P(None, ("gx", "gy", "gz")),
        P(None, ("gx", "gy", "gz"), None),
        P(None, ("gx", "gy", "gz"), None),
        P(None, ("gx", "gy", "gz"), None),
        P(None, None, ("gx", "gy", "gz")),
    )
    out_specs = P(("gx", "gy", "gz"), None)
    return jax.shard_map(body, mesh=mesh, in_specs=in_specs, out_specs=out_specs, check_vma=False)
```

profile of v0, /device:TPU:0, one launch (start us, length us, event | category | flops | bytes accessed | tf_op | source)
XLA Modules:
  0.0 307.4 jit_solution(744721059821343803)
XLA Ops:
  6.5 0.0 copy-start
  6.5 0.0 all-gather.26.cloned.1.call-start
  6.5 12.0 %all-gather.9 = bf16[1,512,512]{2,1,0:T(8,128)(2,1)} all-gather(bf16[1,256,512]{2,1,0:T(8,128)(2,1)} %param.12), channel_id=11, replica_groups=mesh['gx'=4,'gy'=4,'gz'=2] {'gz'}, dimensions={1}, use_global_device_ids=true | all-gather | bytes 786432 | tf_op jit(solution)/shard_map/all_gather | solution.py:44
  18.6 0.0 all-gather.26.cloned.1.call-update
  18.6 0.0 copy-start.3
  18.6 0.0 copy-start.1
  18.6 0.0 all-gather.30.cloned.1.call-start
  18.7 8.5 %all-gather.12 = bf16[1,512,512]{2,1,0:T(8,128)(2,1)} all-gather(bf16[1,512,256]{2,1,0:T(8,128)(2,1)} %param.15), channel_id=14, replica_groups=mesh['gx'=4,'gy'=4,'gz'=2] {'gz'}, dimensions={2}, use_global_device_ids=true | all-gather | bytes 786432 | tf_op jit(solution)/shard_map/all_gather | solution.py:66
  27.1 0.0 all-gather.30.cloned.1.call-update
  27.2 0.0 all-gather.24.cloned.1.call-start
  27.2 5.2 %all-gather.6 = bf16[1,512,128]{2,1,0:T(8,128)(2,1)S(1)} all-gather(bf16[1,256,128]{2,1,0:T(8,128)(2,1)} %param.13), channel_id=8, replica_groups=mesh['gx'=4,'gy'=4,'gz'=2] {'gz'}, dimensions={1}, use_global_device_ids=true | all-gather | bytes 196608 | tf_op jit(solution)/shard_map/all_gather | solution.py:45
  32.4 23.9 %all-gather.7 = bf16[1,2048,128]{2,1,0:T(8,128)(2,1)} all-gather(bf16[1,512,128]{2,1,0:T(8,128)(2,1)S(1)} %all-gather.6), channel_id=9, replica_groups=mesh['gx'=4,'gy'=4,'gz'=2] {'gy'}, dimensions={1}, use_global_device_ids=true | all-gather | bytes 655360 | tf_op jit(solution)/shard_map/all_gather | solution.py:51
  56.2 0.0 all-gather.24.cloned.1.call-update
  56.2 0.0 all-gather.28.cloned.1.call-start
  56.3 16.9 %all-gather.26.cloned.1.call-done = bf16[1,2048,512]{2,1,0:T(8,128)(2,1)} async-done(((bf16[1,512,512]{2,1,0:T(8,128)(2,1)}), bf16[1,2048,512]{2,1,0:T(8,128)(2,1)}) %all-gather.26.cloned.1.call-update) | async-done | bytes 2097168 | tf_op jit(solution)/shard_map/all_gather | solution.py:50
  73.2 0.0 all-gather.28.cloned.1.call-update
  73.2 0.0 copy-start.2
  73.2 0.0 all-gather.22.cloned.1.call-start
  73.2 0.0 copy-done
  73.3 4.9 %all-gather.3 = bf16[1,512,128]{2,1,0:T(8,128)(2,1)S(1)} all-gather(bf16[1,256,128]{2,1,0:T(8,128)(2,1)S(1)} %copy-done), channel_id=5, replica_groups=mesh['gx'=4,'gy'=4,'gz'=2] {'gz'}, dimensions={1}, use_global_device_ids=true | all-gather | bytes 196608 | tf_op jit(solution)/shard_map/all_gather | solution.py:46
  78.2 20.2 %all-gather.4 = bf16[1,2048,128]{2,1,0:T(8,128)(2,1)} all-gather(bf16[1,512,128]{2,1,0:T(8,128)(2,1)S(1)} %all-gather.3), channel_id=6, replica_groups=mesh['gx'=4,'gy'=4,'gz'=2] {'gy'}, dimensions={1}, use_global_device_ids=true | all-gather | bytes 655360 | tf_op jit(solution)/shard_map/all_gather | solution.py:52
  98.4 0.0 all-gather.22.cloned.1.call-update
  98.4 0.0 all-gather.32.cloned.1.call-start
  98.4 26.2 %all-gather.30.cloned.1.call-done = bf16[1,512,2048]{2,1,0:T(8,128)(2,1)} async-done(((bf16[1,512,512]{2,1,0:T(8,128)(2,1)}), bf16[1,512,2048]{2,1,0:T(8,128)(2,1)}) %all-gather.30.cloned.1.call-update) | async-done | bytes 2097168 | tf_op jit(solution)/shard_map/all_gather | solution.py:67
  124.7 0.0 all-gather.32.cloned.1.call-update
  124.7 0.0 copy-done.3
  124.7 4.2 %all-gather = bf16[1,512]{1,0:T(2,128)(2,1)S(1)} all-gather(bf16[1,256]{1,0:T(2,128)(2,1)S(1)} %copy-done.3), channel_id=2, replica_groups=mesh['gx'=4,'gy'=4,'gz'=2] {'gz'}, dimensions={1}, use_global_device_ids=true | all-gather | bytes 1536 | tf_op jit(solution)/shard_map/all_gather | solution.py:43
  128.9 11.9 %all-gather.1 = bf16[1,2048]{1,0:T(2,128)(2,1)S(1)} all-gather(bf16[1,512]{1,0:T(2,128)(2,1)S(1)} %all-gather), channel_id=3, replica_groups=mesh['gx'=4,'gy'=4,'gz'=2] {'gy'}, dimensions={1}, use_global_device_ids=true | all-gather | bytes 5120 | tf_op jit(solution)/shard_map/all_gather | solution.py:49
  140.9 5.5 %all-gather.2 = bf16[1,8192]{1,0:T(2,128)(2,1)S(1)} all-gather(bf16[1,2048]{1,0:T(2,128)(2,1)S(1)} %all-gather.1), channel_id=4, replica_groups=mesh['gx'=4,'gy'=4,'gz'=2] {'gx'}, dimensions={1}, use_global_device_ids=true | all-gather | bytes 20480 | tf_op jit(solution)/shard_map/all_gather | solution.py:54
  146.4 0.0 copy-done.1
  146.4 3.1 %fusion.2 = f32[256]{0:T(256)S(1)} fusion(bf16[256,8192]{1,0:T(8,128)(2,1)} %param.8), kind=kLoop, calls=%fused_computation.5 | loop fusion | flops 6291200 | bytes 4195328 | tf_op jit(solution)/shard_map/reduce_sum | solution.py:40
  149.6 0.0 copy-done.2
  149.6 0.1 compare_and_fusion
  149.7 0.3 multiply_cosine_fusion
  150.0 0.0 all-gather.24.cloned.1.call-done
  150.1 4.6 %fusion.8 = f32[256,128]{0,1:T(8,128)S(1)} fusion(bf16[1,8192,128]{2,1,0:T(8,128)(2,1)} %all-gather.24.cloned.1.call-done, bf16[256,8192]{1,0:T(8,128)(2,1)} %param.8, f32[8192]{0:T(1024)S(1)} %bitcast.83, f32[256]{0:T(256)S(1)} %add_rsqrt_fusion), kind=kOutput, calls=%fused_computation.11 | convolution fusion | flops 545259520 | bytes 6456320 | tf_op jit(solution)/shard_map/dot_general | solution.py:60
  154.7 0.1 copy.10
  154.8 0.1 copy.9
  154.9 52.9 %all-gather.28.cloned.1.call-done = bf16[1,8192,512]{2,1,0:T(8,128)(2,1)} async-done(((bf16[1,2048,512]{2,1,0:T(8,128)(2,1)}), bf16[1,8192,512]{2,1,0:T(8,128)(2,1)}) %all-gather.28.cloned.1.call-update) | async-done | bytes 8388624 | tf_op jit(solution)/shard_map/all_gather | solution.py:55
  207.9 7.0 %fusion.6 = f32[256,512]{1,0:T(8,128)S(1)} fusion(bf16[1,8192,512]{2,1,0:T(8,128)(2,1)} %all-gather.28.cloned.1.call-done, bf16[256,8192]{1,0:T(8,128)(2,1)} %param.8, f32[8192]{0:T(1024)S(1)} %bitcast.84, f32[256]{0:T(256)S(1)} %add_rsqrt_fusion), kind=kOutput, calls=%fused_computation.9 | convolution fusion | flops 2155872256 | bytes 13140992 | tf_op jit(solution)/shard_map/dot_general | solution.py:59
  214.9 0.2 reshape.93
  215.1 0.3 slice_negate_fusion
  215.4 0.4 maximum_multiply_fusion
  215.8 0.1 mul.85
  215.9 0.5 fusion.44
  216.4 15.4 %all-gather.22.cloned.1.call-done = bf16[1,8192,128]{2,1,0:T(8,128)(2,1)} async-done(((bf16[1,2048,128]{2,1,0:T(8,128)(2,1)}), bf16[1,8192,128]{2,1,0:T(8,128)(2,1)}) %all-gather.22.cloned.1.call-update) | async-done | bytes 2097168 | tf_op jit(solution)/shard_map/all_gather | solution.py:57
  231.9 4.7 %convolution_convert_fusion = bf16[128,4,256]{2,0,1:T(8,128)(2,1)S(1)} fusion(bf16[1,8192,128]{2,1,0:T(8,128)(2,1)} %all-gather.22.cloned.1.call-done, f32[4,256,256]{1,2,0:T(8,128)S(1)} %get-tuple-element.15, f32[4,256]{1,0:T(4,128)S(1)} %get-tuple-element.14, bf16[256,8192]{1,0:T(8,128)(2,1)} %param.8, f32[8192]{0:T(1024)S(1)} %bitcast.85, ...), kind=kOutput, calls=%fused_computation.20 | convolution fusion | flops 613056512 | bytes 7640064 | tf_op jit(solution)/shard_map/hts,sd->thd/dot_general | solution.py:31
  236.5 55.0 %all-gather.32.cloned.1.call-done = bf16[1,512,8192]{2,1,0:T(8,128)(2,1)} async-done(((bf16[1,512,2048]{2,1,0:T(8,128)(2,1)}), bf16[1,512,8192]{2,1,0:T(8,128)(2,1)}) %all-gather.32.cloned.1.call-update) | async-done | bytes 8388624 | tf_op jit(solution)/shard_map/all_gather | solution.py:70
  291.6 9.0 %fusion.1 = bf16[256,8192]{1,0:T(8,128)(2,1)} fusion(bf16[256,512]{0,1:T(8,128)(2,1)S(1)} %bitcast.82, bf16[256,8192]{1,0:T(8,128)(2,1)} %param.8, bf16[1,512,8192]{2,1,0:T(8,128)(2,1)} %all-gather.32.cloned.1.call-done), kind=kOutput, calls=%fused_computation.4 | convolution fusion | flops 2153775104 | bytes 17039360 | tf_op jit(solution)/shard_map/dot_general | solution.py:68
  (6 shorter events, 0.1 us)
Async XLA Ops:
  6.5 66.7 %copy-start = (bf16[1,256,128]{2,1,0:T(8,128)(2,1)S(1)}, bf16[1,256,128]{2,1,0:T(8,128)(2,1)}, u32[]{:S(2)}) copy-start(bf16[1,256,128]{2,1,0:T(8,128)(2,1)} %param.14) | copy-start | bytes 196612
  6.5 66.6 %all-gather.26.cloned.1.call-start = ((), (), s32[]{:S(2)}) async-start(), calls=%async_computation.2 | async-start | bytes 2621440 | tf_op jit(solution)/shard_map/all_gather | solution.py:50
  18.6 106.1 %copy-start.3 = (bf16[1,256]{1,0:T(2,128)(2,1)S(1)}, bf16[1,256]{1,0:T(2,128)(2,1)}, u32[]{:S(2)}) copy-start(bf16[1,256]{1,0:T(2,128)(2,1)} %param.11) | copy-start | bytes 1540
  18.6 127.8 %copy-start.1 = (s32[256]{0:T(256)S(1)}, s32[256]{0:T(256)}, u32[]{:S(2)}) copy-start(s32[256]{0:T(256)} %param.10) | copy-start | bytes 3076
  18.6 106.0 %all-gather.30.cloned.1.call-start = ((), (), s32[]{:S(2)}) async-start(), calls=%async_computation.4 | async-start | bytes 2621440 | tf_op jit(solution)/shard_map/all_gather | solution.py:67
  27.2 122.9 %all-gather.24.cloned.1.call-start = ((), (), s32[]{:S(2)}) async-start(), calls=%async_computation.1 | async-start | bytes 2621440 | tf_op jit(solution)/shard_map/all_gather | solution.py:56
  56.2 151.6 %all-gather.28.cloned.1.call-start = ((), (), s32[]{:S(2)}) async-start(), calls=%async_computation.3 | async-start | bytes 10485760 | tf_op jit(solution)/shard_map/all_gather | solution.py:55
  73.2 76.4 %copy-start.2 = (s32[256]{0:T(256)S(1)}, s32[256]{0:T(256)}, u32[]{:S(2)}) copy-start(s32[256]{0:T(256)} %param.9) | copy-start | bytes 3076
  73.2 158.7 %all-gather.22.cloned.1.call-start = ((), (), s32[]{:S(2)}) async-start(), calls=%async_computation | async-start | bytes 2621440 | tf_op jit(solution)/shard_map/all_gather | solution.py:57
  98.4 193.2 %all-gather.32.cloned.1.call-start = ((), (), s32[]{:S(2)}) async-start(), calls=%async_computation.5 | async-start | bytes 10485760 | tf_op jit(solution)/shard_map/all_gather | solution.py:70
Sparse Core Ops, SparseCore 0:
  18.7 54.3 all-gather.25
  74.7 49.8 all-gather.29
  126.2 21.8 all-gather.23
  149.6 58.2 all-gather.27
  209.3 22.5 all-gather.21
  233.3 58.2 all-gather.31
where the time goes:
time: 308 us; the launch traced here: 307 us
  waiting for transfers between devices  167 us (54%)
  blocking collectives  96.3 us (31%)
  matrix products  25.9 us (8%)
  between operations  13.6 us (4%)
  other arithmetic  4.37 us (1%)
    all_gather x1, waiting for transfers between devices, body(): lax.all_gather(middle_cols, 'gx', axis=1, tiled=True)  55 us
    all_gather x1, waiting for transfers between devices, body(): query_piece = lax.all_gather(middle[1], 'gx', axis=0, tiled=True)  52.9 us
    all_gather x1, waiting for transfers between devices, body(): middle_cols = lax.all_gather(inner_cols, 'gy', axis=1, tiled=True)  26.2 us
    all_gather x1, blocking collectives, body(): lax.all_gather(inner[2], 'gy', axis=0, tiled=True)  23.9 us
    all_gather x1, blocking collectives, body(): lax.all_gather(inner[3], 'gy', axis=0, tiled=True)  20.2 us
    all_gather x1, waiting for transfers between devices, body(): lax.all_gather(inner[1], 'gy', axis=0, tiled=True)  16.9 us
    all_gather x1, waiting for transfers between devices, body(): value_piece = lax.all_gather(middle[3], 'gx', axis=0, tiled=True)  15.4 us
    all_gather x1, blocking collectives, body(): lax.all_gather(q_weight[0], 'gz', axis=0, tiled=True)  12 us
  transfers between devices with their start and end apart: 6, of which 5 were waited for; matrix products, arithmetic and copies ran while one was open for 7% of the time, Pallas kernels for 0%

commit v1 on v0

--- a/solution.py
+++ b/solution.py
@@ -64,7 +64,15 @@
     values = value_raw.astype(jnp.bfloat16)
     mixed = attend(queries, keys, values, segment_ids, positions)
     inner_cols = lax.all_gather(o_weight[0], "gz", axis=1, tiled=True)
-    middle_cols = lax.all_gather(inner_cols, "gy", axis=1, tiled=True)
+    axis_total = lax.axis_size("gy")
+    d_next = [(i0 - 1, i0) for i0 in range(1, axis_total)] + [(axis_total - 1, 0)]
+    now = inner_cols
+    in_order = [now]
+    for _ in range(axis_total - 1):
+        now = lax.ppermute(now, axis_name="gy", perm=d_next)
+        in_order += [now]
+    k_now = jnp.concatenate([*reversed(in_order)], axis=1)
+    middle_cols = jnp.roll(k_now, shift=(lax.axis_index("gy") + 1) * now.shape[1], axis=1)
     branch = jnp.dot(
         mixed,
         lax.all_gather(middle_cols, "gx", axis=1, tiled=True),

time: 308 us -> 253 us (0.82)
  waiting for transfers between devices: 167 us -> 116 us
  blocking collectives: 96.3 us -> 89.8 us
    all_gather x1, waiting for transfers between devices: 52.9 us -> 0.02 us  [body(): query_piece = lax.all_gather(middle[1], 'gx', axis=0, tiled=True)]
    ppermute x0 -> x3, waiting for transfers between devices: none -> 35.3 us  [body(): now = lax.ppermute(now, axis_name='gy', perm=d_next)]
    all_gather x1 -> x0, waiting for transfers between devices: 26.2 us -> none  [body(): middle_cols = lax.all_gather(inner_cols, 'gy', axis=1, tiled=True)]
    all_gather x1, waiting for transfers between devices: 15.4 us -> 1.45 us  [body(): value_piece = lax.all_gather(middle[3], 'gx', axis=0, tiled=True)]
    all_gather x1, waiting for transfers between devices: 16.9 us -> 23.8 us  [body(): lax.all_gather(inner[1], 'gy', axis=0, tiled=True)]
    all_gather x1, blocking collectives: 20.2 us -> 16.3 us  [body(): lax.all_gather(inner[3], 'gy', axis=0, tiled=True)]
  transfers between devices with their start and end apart: 6 -> 8, of which waited for: 5 -> 6; matrix products, arithmetic and copies ran while one was open for 7% -> 10% of each run, Pallas kernels for 0% -> 0%
where the time goes in v1:
time: 253 us
  waiting for transfers between devices  116 us (46%)
  blocking collectives  89.8 us (35%)
  matrix products  26.1 us (10%)
  between operations  13.4 us (5%)
  other arithmetic  4.38 us (2%)
  local copies, waits for them, and re-layouts  2.61 us (1%)
    all_gather x1, waiting for transfers between devices, body(): lax.all_gather(middle_cols, 'gx', axis=1, tiled=True)  55 us
    ppermute x3, waiting for transfers between devices, body(): now = lax.ppermute(now, axis_name='gy', perm=d_next)  35.3 us
    all_gather x1, waiting for transfers between devices, body(): lax.all_gather(inner[1], 'gy', axis=0, tiled=True)  23.8 us
    all_gather x1, blocking collectives, body(): lax.all_gather(inner[2], 'gy', axis=0, tiled=True)  23.1 us
    all_gather x1, blocking collectives, body(): lax.all_gather(inner[3], 'gy', axis=0, tiled=True)  16.3 us
    all_gather x1, blocking collectives, body(): lax.all_gather(q_weight[0], 'gz', axis=0, tiled=True)  12 us
    all_gather x1, blocking collectives, body(): lax.all_gather(inner[0], 'gy', axis=0, tiled=True)  11.9 us
    dot_general x1, matrix products, body(): jnp.dot(mixed, lax.all_gather(middle_cols, 'gx', axis=1, tiled=True), pre...  9.02 us
  transfers between devices with their start and end apart: 8, of which 6 were waited for; matrix products, arithmetic and copies ran while one was open for 10% of the time, Pallas kernels for 0%

profile of v1, /device:TPU:0, one launch (start us, length us, event | category | flops | bytes accessed | tf_op | source)
XLA Modules:
  0.0 253.1 jit_solution(4556272814398298820)
XLA Ops:
  6.5 0.0 copy-start.1
  6.5 0.0 copy-start
  6.5 0.0 all-gather.25.cloned.1.call-start
  6.5 12.0 %all-gather.9 = bf16[1,512,512]{2,1,0:T(8,128)(2,1)} all-gather(bf16[1,256,512]{2,1,0:T(8,128)(2,1)} %param.12), channel_id=11, replica_groups=mesh['gx'=4,'gy'=4,'gz'=2] {'gz'}, dimensions={1}, use_global_device_ids=true | all-gather | bytes 786432 | tf_op jit(solution)/shard_map/all_gather | solution.py:44
  18.6 0.0 all-gather.25.cloned.1.call-update
  18.6 0.0 all-gather.23.cloned.1.call-start
  18.6 5.1 %all-gather.6 = bf16[1,512,128]{2,1,0:T(8,128)(2,1)S(1)} all-gather(bf16[1,256,128]{2,1,0:T(8,128)(2,1)} %param.13), channel_id=8, replica_groups=mesh['gx'=4,'gy'=4,'gz'=2] {'gz'}, dimensions={1}, use_global_device_ids=true | all-gather | bytes 196608 | tf_op jit(solution)/shard_map/all_gather | solution.py:45
  23.8 23.1 %all-gather.7 = bf16[1,2048,128]{2,1,0:T(8,128)(2,1)} all-gather(bf16[1,512,128]{2,1,0:T(8,128)(2,1)S(1)} %all-gather.6), channel_id=9, replica_groups=mesh['gx'=4,'gy'=4,'gz'=2] {'gy'}, dimensions={1}, use_global_device_ids=true | all-gather | bytes 655360 | tf_op jit(solution)/shard_map/all_gather | solution.py:51
  46.9 0.0 all-gather.23.cloned.1.call-update
  46.9 0.0 all-gather.27.cloned.1.call-start
  47.0 23.8 %all-gather.25.cloned.1.call-done = bf16[1,2048,512]{2,1,0:T(8,128)(2,1)} async-done(((bf16[1,512,512]{2,1,0:T(8,128)(2,1)}), bf16[1,2048,512]{2,1,0:T(8,128)(2,1)}) %all-gather.25.cloned.1.call-update) | async-done | bytes 2097168 | tf_op jit(solution)/shard_map/all_gather | solution.py:50
  70.8 0.0 all-gather.27.cloned.1.call-update
  70.8 0.0 all-gather.21.cloned.1.call-start
  70.8 0.0 copy-done.1
  70.8 4.9 %all-gather.3 = bf16[1,512,128]{2,1,0:T(8,128)(2,1)S(1)} all-gather(bf16[1,256,128]{2,1,0:T(8,128)(2,1)S(1)} %copy-done.1), channel_id=5, replica_groups=mesh['gx'=4,'gy'=4,'gz'=2] {'gz'}, dimensions={1}, use_global_device_ids=true | all-gather | bytes 196608 | tf_op jit(solution)/shard_map/all_gather | solution.py:46
  75.8 16.3 %all-gather.4 = bf16[1,2048,128]{2,1,0:T(8,128)(2,1)} all-gather(bf16[1,512,128]{2,1,0:T(8,128)(2,1)S(1)} %all-gather.3), channel_id=6, replica_groups=mesh['gx'=4,'gy'=4,'gz'=2] {'gy'}, dimensions={1}, use_global_device_ids=true | all-gather | bytes 655360 | tf_op jit(solution)/shard_map/all_gather | solution.py:52
  92.0 0.0 all-gather.21.cloned.1.call-update
  92.1 0.0 all-gather.19.cloned.1.call-start
  92.1 0.0 copy-done
  92.1 7.0 %all-gather.12 = bf16[1,512,512]{2,1,0:T(8,128)(2,1)S(1)} all-gather(bf16[1,512,256]{2,1,0:T(8,128)(2,1)S(1)} %copy-done), channel_id=14, replica_groups=mesh['gx'=4,'gy'=4,'gz'=2] {'gz'}, dimensions={2}, use_global_device_ids=true | all-gather | bytes 786432 | tf_op jit(solution)/shard_map/all_gather | solution.py:66
  99.2 0.9 collective-permute-start
  100.1 11.2 %collective-permute-done = bf16[512,512]{1,0:T(8,128)(2,1)S(1)} collective-permute-done((bf16[512,512]{1,0:T(8,128)(2,1)S(1)}, bf16[512,512]{1,0:T(8,128)(2,1)S(1)}, u32[]{:S(2)}, u32[]{:S(2)}) %collective-permute-start) | collective-permute-done | bytes 524320 | tf_op jit(solution)/shard_map/ppermute | solution.py:72
  111.3 0.0 collective-permute-start.1
  111.3 12.8 %collective-permute-done.1 = bf16[512,512]{1,0:T(8,128)(2,1)S(1)} collective-permute-done((bf16[512,512]{1,0:T(8,128)(2,1)S(1)}, bf16[512,512]{1,0:T(8,128)(2,1)S(1)}, u32[]{:S(2)}, u32[]{:S(2)}) %collective-permute-start.1) | collective-permute-done | bytes 524320 | tf_op jit(solution)/shard_map/ppermute | solution.py:72
  124.0 0.0 collective-permute-start.2
  124.0 11.3 %collective-permute-done.2 = bf16[512,512]{1,0:T(8,128)(2,1)S(1)} collective-permute-done((bf16[512,512]{1,0:T(8,128)(2,1)S(1)}, bf16[512,512]{1,0:T(8,128)(2,1)S(1)}, u32[]{:S(2)}, u32[]{:S(2)}) %collective-permute-start.2) | collective-permute-done | bytes 524320 | tf_op jit(solution)/shard_map/ppermute | solution.py:72
  135.4 0.1 constant_dynamic-update-slice_fusion.7
  135.4 0.1 constant_dynamic-update-slice_fusion.6
  135.5 0.1 constant_dynamic-update-slice_fusion.5
  135.6 0.1 constant_dynamic-update-slice_fusion.4
  135.7 0.1 constant_dynamic-update-slice_fusion.3
  135.7 0.1 constant_dynamic-update-slice_fusion.2
  135.8 0.0 copy-start.2
  135.8 0.0 copy-start.4
  135.9 0.1 constant_dynamic-update-slice_fusion.1
  135.9 0.1 constant_dynamic-update-slice_fusion
  136.0 1.6 constant_dynamic-slice_fusion
  137.6 0.0 copy-start.3
  137.6 0.0 all-gather.19.cloned.1.call-update
  137.6 0.0 copy-done.2
  137.6 0.0 copy-done.4
  137.6 4.2 %all-gather = bf16[1,512]{1,0:T(2,128)(2,1)S(1)} all-gather(bf16[1,256]{1,0:T(2,128)(2,1)S(1)} %copy-done.4), channel_id=2, replica_groups=mesh['gx'=4,'gy'=4,'gz'=2] {'gz'}, dimensions={1}, use_global_device_ids=true | all-gather | bytes 1536 | tf_op jit(solution)/shard_map/all_gather | solution.py:43
  141.9 11.9 %all-gather.1 = bf16[1,2048]{1,0:T(2,128)(2,1)S(1)} all-gather(bf16[1,512]{1,0:T(2,128)(2,1)S(1)} %all-gather), channel_id=3, replica_groups=mesh['gx'=4,'gy'=4,'gz'=2] {'gy'}, dimensions={1}, use_global_device_ids=true | all-gather | bytes 5120 | tf_op jit(solution)/shard_map/all_gather | solution.py:49
  153.8 5.2 %all-gather.2 = bf16[1,8192]{1,0:T(2,128)(2,1)S(1)} all-gather(bf16[1,2048]{1,0:T(2,128)(2,1)S(1)} %all-gather.1), channel_id=4, replica_groups=mesh['gx'=4,'gy'=4,'gz'=2] {'gx'}, dimensions={1}, use_global_device_ids=true | all-gather | bytes 20480 | tf_op jit(solution)/shard_map/all_gather | solution.py:54
  159.0 3.1 %fusion.2 = f32[256]{0:T(256)S(1)} fusion(bf16[256,8192]{1,0:T(8,128)(2,1)} %param.8), kind=kLoop, calls=%fused_computation.5 | loop fusion | flops 6291200 | bytes 4195328 | tf_op jit(solution)/shard_map/reduce_sum | solution.py:40
  162.2 0.0 copy-done.3
  162.2 0.1 compare_and_fusion
  162.3 0.3 multiply_cosine_fusion
  162.6 0.0 all-gather.23.cloned.1.call-done
  162.7 4.8 %fusion.7 = f32[256,128]{0,1:T(8,128)S(1)} fusion(bf16[1,8192,128]{2,1,0:T(8,128)(2,1)} %all-gather.23.cloned.1.call-done, bf16[256,8192]{1,0:T(8,128)(2,1)} %param.8, f32[8192]{0:T(1024)S(1)} %bitcast.85, f32[256]{0:T(256)S(1)} %add_rsqrt_fusion), kind=kOutput, calls=%fused_computation.10 | convolution fusion | flops 545259520 | bytes 6456320 | tf_op jit(solution)/shard_map/dot_general | solution.py:60
  167.6 0.1 copy.10
  167.7 0.1 copy.9
  167.8 0.0 all-gather.27.cloned.1.call-done
  167.8 7.1 %fusion.5 = f32[256,512]{1,0:T(8,128)S(1)} fusion(bf16[1,8192,512]{2,1,0:T(8,128)(2,1)} %all-gather.27.cloned.1.call-done, bf16[256,8192]{1,0:T(8,128)(2,1)} %param.8, f32[8192]{0:T(1024)S(1)} %bitcast.86, f32[256]{0:T(256)S(1)} %add_rsqrt_fusion), kind=kOutput, calls=%fused_computation.8 | convolution fusion | flops 2155872256 | bytes 13140992 | tf_op jit(solution)/shard_map/dot_general | solution.py:59
  174.9 0.2 reshape.93
  175.1 0.3 slice_negate_fusion
  175.4 0.4 maximum_multiply_fusion
  175.8 0.1 mul.88
  175.9 0.5 fusion.43
  176.4 1.4 all-gather.21.cloned.1.call-done
  177.9 4.7 %convolution_convert_fusion = bf16[128,4,256]{2,0,1:T(8,128)(2,1)S(1)} fusion(bf16[1,8192,128]{2,1,0:T(8,128)(2,1)} %all-gather.21.cloned.1.call-done, f32[4,256,256]{1,2,0:T(8,128)S(1)} %get-tuple-element.15, f32[4,256]{1,0:T(4,128)S(1)} %get-tuple-element.14, bf16[256,8192]{1,0:T(8,128)(2,1)} %param.8, f32[8192]{0:T(1024)S(1)} %bitcast.87, ...), kind=kOutput, calls=%fused_computation.19 | convolution fusion | flops 613056512 | bytes 7640064 | tf_op jit(solution)/shard_map/hts,sd->thd/dot_general | solution.py:31
  182.6 55.0 %all-gather.19.cloned.1.call-done = bf16[512,8192]{1,0:T(8,128)(2,1)} async-done(((bf16[512,2048]{1,0:T(8,128)(2,1)}), bf16[512,8192]{1,0:T(8,128)(2,1)}) %all-gather.19.cloned.1.call-update) | async-done | bytes 8388624 | tf_op jit(solution)/shard_map/all_gather | solution.py:78
  237.6 9.0 %fusion.1 = bf16[256,8192]{1,0:T(8,128)(2,1)} fusion(bf16[256,512]{0,1:T(8,128)(2,1)S(1)} %bitcast.84, bf16[512,8192]{1,0:T(8,128)(2,1)} %all-gather.19.cloned.1.call-done, bf16[256,8192]{1,0:T(8,128)(2,1)} %param.8), kind=kOutput, calls=%fused_computation.4 | convolution fusion | flops 2153775104 | bytes 17039360 | tf_op jit(solution)/shard_map/dot_general | solution.py:76
  (6 shorter events, 0.1 us)
Async XLA Ops:
  6.5 64.3 %copy-start.1 = (bf16[1,256,128]{2,1,0:T(8,128)(2,1)S(1)}, bf16[1,256,128]{2,1,0:T(8,128)(2,1)}, u32[]{:S(2)}) copy-start(bf16[1,256,128]{2,1,0:T(8,128)(2,1)} %param.14) | copy-start | bytes 196612
  6.5 85.6 %copy-start = (bf16[1,512,256]{2,1,0:T(8,128)(2,1)S(1)}, bf16[1,512,256]{2,1,0:T(8,128)(2,1)}, u32[]{:S(2)}) copy-start(bf16[1,512,256]{2,1,0:T(8,128)(2,1)} %param.15) | copy-start | bytes 786436
  6.5 64.2 %all-gather.25.cloned.1.call-start = ((), (), s32[]{:S(2)}) async-start(), calls=%async_computation.3 | async-start | bytes 2621440 | tf_op jit(solution)/shard_map/all_gather | solution.py:50
  18.6 144.1 %all-gather.23.cloned.1.call-start = ((), (), s32[]{:S(2)}) async-start(), calls=%async_computation.2 | async-start | bytes 2621440 | tf_op jit(solution)/shard_map/all_gather | solution.py:56
  46.9 120.9 %all-gather.27.cloned.1.call-start = ((), (), s32[]{:S(2)}) async-start(), calls=%async_computation.4 | async-start | bytes 10485760 | tf_op jit(solution)/shard_map/all_gather | solution.py:55
  70.8 107.1 %all-gather.21.cloned.1.call-start = ((), (), s32[]{:S(2)}) async-start(), calls=%async_computation.1 | async-start | bytes 2621440 | tf_op jit(solution)/shard_map/all_gather | solution.py:57
  92.1 145.5 %all-gather.19.cloned.1.call-start = ((), (), s32[]{:S(2)}) async-start(), calls=%async_computation | async-start | bytes 10485760 | tf_op jit(solution)/shard_map/all_gather | solution.py:78
  99.2 12.1 %collective-permute-start = (bf16[512,512]{1,0:T(8,128)(2,1)S(1)}, bf16[512,512]{1,0:T(8,128)(2,1)S(1)}, u32[]{:S(2)}, u32[]{:S(2)}) collective-permute-start(bf16[512,512]{1,0:T(8,128)(2,1)S(1)} %bitcast.80), channel_id=1, source_target_pairs={{0,2},{2,4},{4,6},{6,0},{1,3},{3,5},{5,7},{7,1},{8,10},{10,12},{12... | collective-permute-start | bytes 1572872 | tf_op jit(solution)/shard_map/ppermute | solution.py:72
  111.3 12.8 %collective-permute-start.1 = (bf16[512,512]{1,0:T(8,128)(2,1)S(1)}, bf16[512,512]{1,0:T(8,128)(2,1)S(1)}, u32[]{:S(2)}, u32[]{:S(2)}) collective-permute-start(bf16[512,512]{1,0:T(8,128)(2,1)S(1)} %collective-permute-done), channel_id=1, source_target_pairs={{0,2},{2,4},{4,6},{6,0},{1,3},{3,5},{5,7},{7,1},{8,10},{10,12},{12... | collective-permute-start | bytes 1572872 | tf_op jit(solution)/shard_map/ppermute | solution.py:72
  124.0 11.3 %collective-permute-start.2 = (bf16[512,512]{1,0:T(8,128)(2,1)S(1)}, bf16[512,512]{1,0:T(8,128)(2,1)S(1)}, u32[]{:S(2)}, u32[]{:S(2)}) collective-permute-start(bf16[512,512]{1,0:T(8,128)(2,1)S(1)} %collective-permute-done.1), channel_id=1, source_target_pairs={{0,2},{2,4},{4,6},{6,0},{1,3},{3,5},{5,7},{7,1},{8,10},{10,12},{12... | collective-permute-start | bytes 1572872 | tf_op jit(solution)/shard_map/ppermute | solution.py:72
  135.8 1.8 copy-start.2
  135.8 1.8 copy-start.4
  137.6 24.6 %copy-start.3 = (s32[256]{0:T(256)S(1)}, s32[256]{0:T(256)}, u32[]{:S(2)}) copy-start(s32[256]{0:T(256)} %param.9) | copy-start | bytes 3076
Sparse Core Ops, SparseCore 0:
  18.7 51.9 all-gather.24
  72.3 21.6 all-gather.22
  95.6 58.2 all-gather.26
  155.3 22.5 all-gather.20
  179.3 58.2 all-gather.18
